TPU v7x, 32 devices: a whole 2x2x4 slice. The times are simulated.
32 devices in a mesh: seq: 2 (over y), section: 4 (over x, core), tp: 4 (over z).
Axes of the slice: x: 2, y: 2, z: 4, core: 2. Of those that a mesh axis runs over, the one named last changes fastest.
Arguments:
- token_ids: int32 [128], P('seq'), may hold values from 0 to 65535
- embed_columns: bfloat16 [4096, 65536], P(('tp', 'seq')), may hold values from -6 to 6
- norm_gain: bfloat16 [4, 4096], P('section'), may hold values from 0.099609375 to 1.8984375
- qkv_weight: bfloat16 [4, 4096, 4096], P('section', 'seq', 'tp'), may hold values from -1 to 1
- out_weight: bfloat16 [4, 4096, 2048], P('section', 'seq', 'tp'), may hold values from -0.125 to 0.125
Outputs:
- layer_states: bfloat16 [4, 128, 4096], P('section', 'seq', 'tp')
All inputs are finite; a program needn't handle non-finite values.
Results may differ from a plain program's by a relative error of at most 0.02.
Values may be sent and summed in bfloat16 or wider, within the bound.
A program may use at most 192 MiB of HBM per device.

v0:
```python
import jax
import jax.numpy as jnp
from jax import lax
from jax.sharding import PartitionSpec as P

QUERY_HEADS = 16
KEY_VALUE_HEADS = 8
HEAD_WIDTH = 128


EPS = 1e-05
ROPE_BASE = 500000.0
MASKED = -1e30


def passed_along(value, axis, steps):
    count = lax.axis_size(axis)
    leading, last = (max(0, -steps), min(count, count - steps))
    return lax.ppermute(value, axis, [(source, source + steps) for source in range(leading, last)])


def from_root(value, axis, root):
    mine = lax.axis_index(axis) == root
    return lax.psum(jnp.where(mine, value, jnp.zeros_like(value)), axis)


def rope_tables(positions, head_size):
    half_width = head_size // 2
    inverse_freq = ROPE_BASE ** (-jnp.arange(half_width).astype(jnp.float32) * (2.0 / head_size))
    angles = positions.astype(jnp.float32)[:, None] * inverse_freq[None, :]
    return (jnp.cos(angles), jnp.sin(angles))


def rotate_half(heads, cosine_table, sine_values):
    half_width = heads.shape[-1] // 2
    first_half = heads[..., :half_width]
    second = heads[..., half_width:]
    cosine_table = cosine_table[:, None, :]
    sine_values = sine_values[:, None, :]
    return jnp.concatenate(
        [
            first_half * cosine_table - second * sine_values,
            second * cosine_table + first_half * sine_values,
        ],
        axis=-1,
    )


def norm_rows(row_block, gain_row):
    values = row_block.astype(jnp.float32)
    inverse_rms = lax.rsqrt(jnp.mean(values * values, axis=-1, keepdims=True) + EPS)
    return (values * inverse_rms * gain_row[None, :]).astype(jnp.bfloat16)


def widen(current):
    return lax.all_gather(current, "tp", axis=1, tiled=True)


def project(full_rows, gain_row, qkv_full, positions, query_heads, key_value_heads):
    row_count = full_rows.shape[0]
    normed = norm_rows(full_rows, gain_row)
    projected_rows = jnp.dot(normed, qkv_full, preferred_element_type=jnp.float32)
    projected_rows = projected_rows.reshape(
        row_count, query_heads + 2 * key_value_heads, HEAD_WIDTH
    )
    cosine_table, sine_values = rope_tables(positions, HEAD_WIDTH)
    query_rows = rotate_half(projected_rows[:, :query_heads], cosine_table, sine_values).astype(
        jnp.bfloat16
    )
    key_head_rows = rotate_half(
        projected_rows[:, query_heads : query_heads + key_value_heads], cosine_table, sine_values
    ).astype(jnp.bfloat16)
    value_head_rows = projected_rows[:, query_heads + key_value_heads :].astype(jnp.bfloat16)
    return (query_rows, key_head_rows, value_head_rows)


def attend(query_rows, key_head_rows, value_head_rows, allowed):
    row_count, query_heads, head_size = query_rows.shape
    key_value_heads = key_head_rows.shape[1]
    query_groups = query_rows.reshape(
        row_count, key_value_heads, query_heads // key_value_heads, head_size
    )
    scores = jnp.einsum(
        "rkph,ckh->kprc", query_groups, key_head_rows, preferred_element_type=jnp.float32
    ) * head_size ** (-0.5)
    scores = jnp.where(allowed[None, None], scores, MASKED)
    weights = jax.nn.softmax(scores, axis=-1).astype(jnp.bfloat16)
    attended = jnp.einsum(
        "kprc,ckh->rkph", weights, value_head_rows, preferred_element_type=jnp.float32
    )
    return attended.reshape(row_count, query_heads * head_size).astype(jnp.bfloat16)


def combine(current, attended, out_full):
    partial_value = lax.dot_general(
        attended, out_full, (((1,), (1,)), ((), ())), preferred_element_type=jnp.float32
    )
    summed = lax.psum_scatter(
        partial_value.astype(jnp.bfloat16), "tp", scatter_dimension=1, tiled=True
    ).astype(jnp.float32)
    return (current.astype(jnp.float32) + summed).astype(jnp.bfloat16)


def advance(new_rows):
    return passed_along(new_rows, "section", 1)


def body(token_ids, embed_columns, norm_gain, qkv_weight, out_weight):
    seq_count = lax.axis_size("seq")
    section_count = lax.axis_size("section")
    tensor_parallel_count = lax.axis_size("tp")
    group_index = lax.axis_index("seq")
    section_index = lax.axis_index("section")
    block_row_slice = token_ids.shape[0]
    feature_slice = embed_columns.shape[0]
    feature_cols = feature_slice * seq_count
    query_heads = QUERY_HEADS // tensor_parallel_count
    key_value_heads = KEY_VALUE_HEADS // tensor_parallel_count
    every_id = lax.all_gather(token_ids, "seq", axis=0, tiled=True)
    looked = jnp.take(embed_columns, every_id, axis=1)
    arrived = lax.all_to_all(looked, "seq", split_axis=1, concat_axis=0, tiled=True)
    residual = arrived.T
    qkv_full, out_full = (
        lax.all_gather(qkv_weight, "seq", axis=1, tiled=True),
        lax.all_gather(out_weight, "seq", axis=1, tiled=True),
    )
    qkv_full = qkv_full[0]
    out_full = out_full[0]
    gain_row = norm_gain[0].astype(jnp.float32)
    outputs = jnp.zeros((block_row_slice, feature_cols), jnp.bfloat16)
    row_ids = jnp.arange(block_row_slice)[:, None]
    column = jnp.arange(2 * block_row_slice)[None, :]
    positions = group_index * block_row_slice + jnp.arange(block_row_slice)
    allowed = jnp.where(
        column < block_row_slice, group_index > 0, column - block_row_slice <= row_ids
    )
    current = residual
    for step_number in range(section_count):
        query_rows, key_head_rows, value_head_rows = project(
            widen(current), gain_row, qkv_full, positions, query_heads, key_value_heads
        )
        anchor_heads, anchor_values = (
            from_root(key_head_rows, "seq", 0),
            from_root(value_head_rows, "seq", 0),
        )
        both_keys = jnp.concatenate([anchor_heads, key_head_rows], axis=0)
        both_values = jnp.concatenate([anchor_values, value_head_rows], axis=0)
        attended = attend(query_rows, both_keys, both_values, allowed)
        new_rows = combine(current, attended, out_full)
        outputs = jnp.where(section_index == step_number, new_rows, outputs)
        if step_number + 1 < section_count:
            current = advance(new_rows)
    return outputs[None]


def solution(mesh):
    placed = (
        P("seq"),
        P(("tp", "seq"), None),
        P("section", None),
        P("section", "seq", "tp"),
        P("section", "seq", "tp"),
    )
    return jax.shard_map(
        body, mesh=mesh, in_specs=placed, out_specs=P("section", "seq", "tp"), check_vma=False
    )
```

profile of v0, /device:TPU:15, one launch (start us, length us, event | category | flops | bytes accessed | tf_op | source)
XLA Modules:
  0.0 493.6 jit_solution(5250696001412698357)
XLA Ops:
  6.5 0.7 all-gather.3.cloned.1.call-update
  7.3 87.0 %copy.18 = bf16[512,65536]{0,1:T(8,128)(2,1)} copy(bf16[512,65536]{1,0:T(8,128)(2,1)} %param.6) | data formatting | bytes 134217728 | tf_op args[1]
  95.8 3.7 all-reduce
  99.7 2.0 gather_fusion
  101.6 0.7 broadcast_select_fusion
  102.4 3.6 all-to-all-start
  106.2 3.7 all-to-all-done
  109.9 12.2 %all_gather.22 = bf16[64,4096]{1,0:T(8,128)(2,1)S(1)} all-gather(bf16[64,1024]{1,0:T(8,128)(2,1)S(1)} %bitcast.203), channel_id=1, replica_groups=mesh['seq'=2,'section'=4,'tp'=4] {'tp'}, dimensions={1}, use_global_device_ids=true | all-gather | bytes 655360 | tf_op jit(solution)/shard_map/all_gather | solution.py:56
  122.3 11.3 %copy.20 = bf16[1024,4096]{1,0:T(8,128)(2,1)} copy(bf16[1024,4096]{0,1:T(8,128)(2,1)} %bitcast.202) | data formatting | bytes 16777216 | tf_op jit(solution)/shard_map/dot_general | solution.py:62
  133.6 6.0 %fusion.50 = f32[64,8,128]{2,0,1:T(8,128)S(1)} fusion(bf16[8,128,4096]{2,1,0:T(8,128)(2,1)} %bitcast.198, bf16[64,4096]{1,0:T(8,128)(2,1)S(1)} %all_gather.22, f32[4096]{0:T(1024)S(1)} %bitcast.207, f32[64]{0:T(128)S(1)} %add_rsqrt_fusion.3), kind=kOutput, calls=%fused_computation.68 | convolution fusion | flops 537919488 | bytes 9191680 | tf_op jit(solution)/shard_map/dot_general | solution.py:62
  139.8 0.7 broadcast_select_fusion.4
  141.4 24.5 %all-reduce.16.cloned.1.call-done = (bf16[64,2,128]{2,0,1:T(8,128)(2,1)}, bf16[64,2,128]{2,0,1:T(8,128)(2,1)}) async-done(((bf16[64,2,128]{2,0,1:T(8,128)(2,1)}, bf16[64,2,128]{2,0,1:T(8,128)(2,1)}), (bf16[64,2,128]{2,0,1:T(8,128)(2,1)}, bf16[64,2,128]{2,0,1:T(8,128)(2,1)})) %all-reduce.16.cloned.1.call-update) | async-done | bytes 65552 | tf_op jit(solution)/shard_map/psum | solution.py:24
  166.0 1.2 fusion.191
  167.1 1.4 fusion.24
  168.6 55.9 %all-gather.5.cloned.1.call-done = bf16[1,4096,512]{2,1,0:T(8,128)(2,1)} async-done(((bf16[1,2048,512]{2,1,0:T(8,128)(2,1)}), bf16[1,4096,512]{2,1,0:T(8,128)(2,1)}) %all-gather.5.cloned.1.call-update) | async-done | bytes 4194320 | tf_op jit(solution)/shard_map/all_gather | solution.py:125
  224.6 4.4 convolution_convert_fusion.3
  229.0 18.8 %reduce-scatter.5.cloned.1.call-done = bf16[64,1024]{1,0:T(8,128)(2,1)} async-done(((bf16[64,4096]{1,0:T(8,128)(2,1)}), bf16[64,1024]{1,0:T(8,128)(2,1)}) %reduce-scatter.5.cloned.1.call-update) | async-done | bytes 131088 | tf_op jit(solution)/shard_map/reduce_scatter | solution.py:98
  247.9 0.9 add_convert_fusion.3
  248.8 1.3 collective-permute-start
  250.1 3.1 collective-permute-done
  253.2 13.0 %all_gather.25 = bf16[64,4096]{1,0:T(8,128)(2,1)S(1)} all-gather(bf16[64,1024]{1,0:T(8,128)(2,1)S(1)} %collective-permute-done), channel_id=1, replica_groups=mesh['seq'=2,'section'=4,'tp'=4] {'tp'}, dimensions={1}, use_global_device_ids=true | all-gather | bytes 655360 | tf_op jit(solution)/shard_map/all_gather | solution.py:56
  266.5 6.1 %fusion.47 = f32[64,8,128]{2,0,1:T(8,128)S(1)} fusion(bf16[8,128,4096]{2,1,0:T(8,128)(2,1)} %bitcast.199, bf16[64,4096]{1,0:T(8,128)(2,1)S(1)} %all_gather.25, f32[64]{0:T(128)S(1)} %add_rsqrt_fusion.2, f32[4096]{0:T(1024)S(1)} %bitcast.208), kind=kOutput, calls=%fused_computation.66 | convolution fusion | flops 537919488 | bytes 9191680 | tf_op jit(solution)/shard_map/dot_general | solution.py:62
  274.1 26.5 %all-reduce.14.cloned.1.call-done = (bf16[64,2,128]{2,0,1:T(8,128)(2,1)}, bf16[64,2,128]{2,0,1:T(8,128)(2,1)}) async-done(((bf16[64,2,128]{2,0,1:T(8,128)(2,1)}, bf16[64,2,128]{2,0,1:T(8,128)(2,1)}), (bf16[64,2,128]{2,0,1:T(8,128)(2,1)}, bf16[64,2,128]{2,0,1:T(8,128)(2,1)})) %all-reduce.14.cloned.1.call-update) | async-done | bytes 65552 | tf_op jit(solution)/shard_map/psum | solution.py:24
  300.7 1.2 fusion.194
  301.8 1.4 fusion.25
  303.3 4.4 convolution_convert_fusion.2
  307.8 19.0 %reduce-scatter.7.cloned.1.call-done = bf16[64,1024]{1,0:T(8,128)(2,1)} async-done(((bf16[64,4096]{1,0:T(8,128)(2,1)}), bf16[64,1024]{1,0:T(8,128)(2,1)}) %reduce-scatter.7.cloned.1.call-update) | async-done | bytes 131088 | tf_op jit(solution)/shard_map/reduce_scatter | solution.py:98
  326.8 0.9 add_convert_fusion.2
  327.7 1.3 collective-permute-start.1
  329.0 3.2 collective-permute-done.1
  332.3 13.2 %all_gather.26 = bf16[64,4096]{1,0:T(8,128)(2,1)S(1)} all-gather(bf16[64,1024]{1,0:T(8,128)(2,1)S(1)} %collective-permute-done.1), channel_id=1, replica_groups=mesh['seq'=2,'section'=4,'tp'=4] {'tp'}, dimensions={1}, use_global_device_ids=true | all-gather | bytes 655360 | tf_op jit(solution)/shard_map/all_gather | solution.py:56
  345.7 6.1 %fusion.44 = f32[64,8,128]{2,0,1:T(8,128)S(1)} fusion(bf16[8,128,4096]{2,1,0:T(8,128)(2,1)} %bitcast.200, bf16[64,4096]{1,0:T(8,128)(2,1)S(1)} %all_gather.26, f32[64]{0:T(128)S(1)} %add_rsqrt_fusion.1, f32[4096]{0:T(1024)S(1)} %bitcast.209), kind=kOutput, calls=%fused_computation.64 | convolution fusion | flops 537919488 | bytes 9191680 | tf_op jit(solution)/shard_map/dot_general | solution.py:62
  353.4 26.6 %all-reduce.12.cloned.1.call-done = (bf16[64,2,128]{2,0,1:T(8,128)(2,1)}, bf16[64,2,128]{2,0,1:T(8,128)(2,1)}) async-done(((bf16[64,2,128]{2,0,1:T(8,128)(2,1)}, bf16[64,2,128]{2,0,1:T(8,128)(2,1)}), (bf16[64,2,128]{2,0,1:T(8,128)(2,1)}, bf16[64,2,128]{2,0,1:T(8,128)(2,1)})) %all-reduce.12.cloned.1.call-update) | async-done | bytes 65552 | tf_op jit(solution)/shard_map/psum | solution.py:24
  380.0 1.2 fusion.197
  381.1 1.4 fusion.26
  382.6 4.4 convolution_convert_fusion.1
  387.1 19.2 %reduce-scatter.9.cloned.1.call-done = bf16[64,1024]{1,0:T(8,128)(2,1)} async-done(((bf16[64,4096]{1,0:T(8,128)(2,1)}), bf16[64,1024]{1,0:T(8,128)(2,1)}) %reduce-scatter.9.cloned.1.call-update) | async-done | bytes 131088 | tf_op jit(solution)/shard_map/reduce_scatter | solution.py:98
  406.3 0.9 add_convert_fusion.1
  407.2 1.3 collective-permute-start.2
  408.5 3.0 collective-permute-done.2
  411.5 13.1 %all_gather.27 = bf16[64,4096]{1,0:T(8,128)(2,1)S(1)} all-gather(bf16[64,1024]{1,0:T(8,128)(2,1)S(1)} %collective-permute-done.2), channel_id=1, replica_groups=mesh['seq'=2,'section'=4,'tp'=4] {'tp'}, dimensions={1}, use_global_device_ids=true | all-gather | bytes 655360 | tf_op jit(solution)/shard_map/all_gather | solution.py:56
  424.8 6.1 %fusion.41 = f32[64,8,128]{2,0,1:T(8,128)S(1)} fusion(bf16[8,128,4096]{2,1,0:T(8,128)(2,1)} %bitcast.201, bf16[64,4096]{1,0:T(8,128)(2,1)S(1)} %all_gather.27, f32[64]{0:T(128)S(1)} %add_rsqrt_fusion, f32[4096]{0:T(1024)S(1)} %bitcast.210), kind=kOutput, calls=%fused_computation.62 | convolution fusion | flops 537919488 | bytes 9191680 | tf_op jit(solution)/shard_map/dot_general | solution.py:62
  432.5 26.6 %all-reduce.10.cloned.1.call-done = (bf16[64,2,128]{2,0,1:T(8,128)(2,1)}, bf16[64,2,128]{2,0,1:T(8,128)(2,1)}) async-done(((bf16[64,2,128]{2,0,1:T(8,128)(2,1)}, bf16[64,2,128]{2,0,1:T(8,128)(2,1)}), (bf16[64,2,128]{2,0,1:T(8,128)(2,1)}, bf16[64,2,128]{2,0,1:T(8,128)(2,1)})) %all-reduce.10.cloned.1.call-update) | async-done | bytes 65552 | tf_op jit(solution)/shard_map/psum | solution.py:24
  459.0 1.2 fusion.200
  460.2 1.4 fusion.27
  461.7 4.4 convolution_convert_fusion
  466.1 19.1 %reduce-scatter.11.cloned.1.call-done = bf16[64,1024]{1,0:T(8,128)(2,1)} async-done(((bf16[64,4096]{1,0:T(8,128)(2,1)}), bf16[64,1024]{1,0:T(8,128)(2,1)}) %reduce-scatter.11.cloned.1.call-update) | async-done | bytes 131088 | tf_op jit(solution)/shard_map/reduce_scatter | solution.py:98
  485.1 1.6 fusion.61
  (71 shorter events, 8.4 us)
Async XLA Ops:
  6.5 115.8 %all-gather.3.cloned.1.call-start = ((), (), s32[]{:S(2)}) async-start(), calls=%async_computation.5 | async-start | bytes 12582912 | tf_op jit(solution)/shard_map/all_gather | solution.py:124
  7.3 87.1 %copy-start.2 = (u32[32]{0:T(128)S(1)}, u32[32]{0:T(128)}, u32[]{:S(2)}) copy-start(u32[32]{0:T(128)} %constant.68) | copy-start | bytes 388
  7.3 88.3 %copy-start.1 = (s32[64]{0:T(128)S(1)}, s32[64]{0:T(128)}, u32[]{:S(2)}) copy-start(s32[64]{0:T(128)} %param.5) | copy-start | bytes 772
  7.3 98.9 %copy-start = (bf16[1,4096]{1,0:T(2,128)(2,1)S(1)}, bf16[1,4096]{1,0:T(2,128)(2,1)}, u32[]{:S(2)}) copy-start(bf16[1,4096]{1,0:T(2,128)(2,1)} %param.7) | copy-start | bytes 24580
  102.4 7.6 %all-to-all-start = ((bf16[512,2,64]{0,2,1:T(8,128)(2,1)}), bf16[512,2,64]{0,2,1:T(8,128)(2,1)S(1)}, u32[]{:S(2)}, u32[]{:S(2)}) async-start(bf16[512,2,64]{0,2,1:T(8,128)(2,1)} %broadcast_select_fusion), calls=%async_computation | async-start | bytes 262144 | tf_op jit(solution)/shard_map/all_to_all | solution.py:121
  105.9 60.0 %all-reduce.16.cloned.1.call-start = ((), (), s32[]{:S(2)}) async-start(), calls=%async_computation.14 | async-start | bytes 131072 | tf_op jit(solution)/shard_map/psum | solution.py:24
  140.5 84.1 %all-gather.5.cloned.1.call-start = ((), (), s32[]{:S(2)}) async-start(), calls=%async_computation.6 | async-start | bytes 6291456 | tf_op jit(solution)/shard_map/all_gather | solution.py:125
  141.2 106.6 %reduce-scatter.5.cloned.1.call-start = ((), (), s32[]{:S(2)}) async-start(), calls=%async_computation.7 | async-start | bytes 655360 | tf_op jit(solution)/shard_map/reduce_scatter | solution.py:98
  229.0 71.7 %all-reduce.14.cloned.1.call-start = ((), (), s32[]{:S(2)}) async-start(), calls=%async_computation.13 | async-start | bytes 131072 | tf_op jit(solution)/shard_map/psum | solution.py:24
  248.8 4.4 collective-permute-start
  274.0 52.8 %reduce-scatter.7.cloned.1.call-start = ((), (), s32[]{:S(2)}) async-start(), calls=%async_computation.8 | async-start | bytes 655360 | tf_op jit(solution)/shard_map/reduce_scatter | solution.py:98
  307.7 72.2 %all-reduce.12.cloned.1.call-start = ((), (), s32[]{:S(2)}) async-start(), calls=%async_computation.12 | async-start | bytes 131072 | tf_op jit(solution)/shard_map/psum | solution.py:24
  327.7 4.5 collective-permute-start.1
  353.2 53.0 %reduce-scatter.9.cloned.1.call-start = ((), (), s32[]{:S(2)}) async-start(), calls=%async_computation.9 | async-start | bytes 655360 | tf_op jit(solution)/shard_map/reduce_scatter | solution.py:98
  387.0 72.0 %all-reduce.10.cloned.1.call-start = ((), (), s32[]{:S(2)}) async-start(), calls=%async_computation.11 | async-start | bytes 131072 | tf_op jit(solution)/shard_map/psum | solution.py:24
  407.2 4.3 collective-permute-start.2
  432.3 52.8 %reduce-scatter.11.cloned.1.call-start = ((), (), s32[]{:S(2)}) async-start(), calls=%async_computation.10 | async-start | bytes 655360 | tf_op jit(solution)/shard_map/reduce_scatter | solution.py:98
Sparse Core Ops, SparseCore 0:
  8.9 105.4 all-gather.2
  140.6 25.3 all-reduce.15
  167.5 57.0 all-gather.4
  229.1 18.7 reduce-scatter.4
  274.1 26.5 all-reduce.13
  307.9 18.8 reduce-scatter.6
  353.3 26.5 all-reduce.11
  387.1 19.0 reduce-scatter.8
  432.4 26.5 all-reduce.9
  466.2 18.8 reduce-scatter.10
where the time goes:
time: 503 us; the launch traced here: 494 us
  waiting for transfers between devices  251 us (50%)
  local copies, waits for them, and re-layouts  102 us (20%)
  blocking collectives  55.2 us (11%)
  matrix products  51.9 us (10%)
  between operations  14.5 us (3%)
  other arithmetic  11.7 us (2%)
  starting transfers between devices  7.78 us (2%)
    psum x4, waiting for transfers between devices, from_root(): return lax.psum(jnp.where(mine, value, jnp.zeros_like(value)), axis)  104 us
    unnamed x10, local copies, waits for them, and re-layouts  87.9 us
    reduce_scatter x4, waiting for transfers between devices, combine(): lax.psum_scatter(partial_value.astype(jnp.bfloat16), 'tp', scatter_dimens...  76.1 us
    all_gather x1, waiting for transfers between devices, body(): lax.all_gather(out_weight, 'seq', axis=1, tiled=True)  55.9 us
    all_gather x4, blocking collectives, widen(): return lax.all_gather(current, 'tp', axis=1, tiled=True)  51.5 us
    dot_general x4, matrix products, project(): jnp.dot(normed, qkv_full, preferred_element_type=jnp.float32)  24.2 us
    dot_general x4, matrix products, combine(): lax.dot_general(attended, out_full, (((1,), (1,)), ((), ())), preferred_e...  17.5 us
    dot_general x1, local copies, waits for them, and re-layouts, project(): jnp.dot(normed, qkv_full, preferred_element_type=jnp.float32)  11.3 us
  transfers between devices with their start and end apart: 14, of which 13 were waited for; matrix products, arithmetic and copies ran while one was open for 19% of the time, Pallas kernels for 0%

commit v1 on v0

--- a/solution.py
+++ b/solution.py
@@ -1,6 +1,10 @@
+import functools
+
 import jax
 import jax.numpy as jnp
 from jax import lax
+from jax.experimental import pallas as pl
+from jax.experimental.pallas import tpu as pltpu
 from jax.sharding import PartitionSpec as P
 
 QUERY_HEADS = 16
@@ -153,7 +157,391 @@
     return outputs[None]
 
 
+LANES = 128
+TOKEN_GROUP = 8
+MESH = pl.DeviceIdType.MESH
+
+
+def lookup_kernel(ids_ref, table_ref, out_ref, tiles, sems):
+    count = out_ref.shape[0]
+    width = table_ref.shape[0]
+    first = lax.axis_index("section") * count
+
+    def fetch(i):
+        start = pl.multiple_of((ids_ref[first + i] // LANES) * LANES, LANES)
+        return pltpu.make_async_copy(
+            table_ref.at[:, pl.ds(start, LANES)], tiles.at[:, pl.ds(i * LANES, LANES)], sems.at[i]
+        )
+
+    for i in range(count):
+        fetch(i).start()
+    rows = lax.broadcasted_iota(jnp.int32, (LANES, LANES), 0)
+    columns = lax.broadcasted_iota(jnp.int32, (LANES, LANES), 1)
+    total = jnp.zeros((width, LANES), jnp.float32)
+    group = min(TOKEN_GROUP, count)
+    for base in range(0, count, group):
+        picks = []
+        for i in range(base, base + group):
+            chosen = jnp.logical_and(rows == ids_ref[first + i] % LANES, columns == i)
+            picks.append(jnp.where(chosen, 1.0, 0.0).astype(jnp.bfloat16))
+        pick = jnp.concatenate(picks, axis=0)
+        for i in range(base, base + group):
+            fetch(i).wait()
+        total += jnp.dot(
+            tiles[:, base * LANES : (base + group) * LANES], pick, preferred_element_type=jnp.float32
+        )
+    out_ref[...] = total.T[:count].astype(jnp.bfloat16)
+
+
+def chain_kernel(
+    n_seq,
+    n_sec,
+    n_tp,
+    piece_ref,
+    gain_ref,
+    cos_ref,
+    sin_ref,
+    qkv_ref,
+    outw_ref,
+    out_ref,
+    wq,
+    wo,
+    hidden,
+    acc,
+    part_send,
+    part_recv,
+    sq_send,
+    sq_recv,
+    heads,
+    rs_send,
+    rs_recv,
+    fresh,
+    w_sem,
+    h_ssem,
+    h_rsem,
+    p_ssem,
+    p_rsem,
+    q_ssem,
+    q_rsem,
+    r_ssem,
+    r_rsem,
+    o_ssem,
+    o_rsem,
+):
+    seq, sec, tp = (lax.axis_index(a) for a in ("seq", "section", "tp"))
+    other = 1 - seq
+    tokens, chunk = fresh.shape
+    piece = tokens // n_sec
+    block = out_ref.shape[1]
+    groups, _, group_width = part_send.shape
+    query_heads = QUERY_HEADS // n_tp
+    kv_heads = KEY_VALUE_HEADS // n_tp
+
+    load_q = [
+        pltpu.make_async_copy(
+            qkv_ref.at[0, pl.ds(((tp + d) % n_tp) * chunk, chunk), :],
+            wq.at[pl.ds(((tp + d) % n_tp) * chunk, chunk), :],
+            w_sem.at[d],
+        )
+        for d in range(n_tp)
+    ]
+    load_o = pltpu.make_async_copy(outw_ref.at[0], wo, w_sem.at[n_tp])
+    for c in load_q:
+        c.start()
+    load_o.start()
+
+    shard = tp * n_seq + seq
+    half, slot = shard // n_tp, shard % n_tp
+
+    def seed_copy(j):
+        return pltpu.make_async_remote_copy(
+            src_ref=piece_ref,
+            dst_ref=hidden.at[slot, pl.ds(sec * piece, piece), :],
+            send_sem=h_ssem.at[0, j],
+            recv_sem=h_rsem.at[slot, sec],
+            device_id={"seq": half, "section": 0, "tp": j},
+            device_id_type=MESH,
+        )
+
+    def seed_is_mine(j):
+        return jnp.logical_and(sec == 0, jnp.logical_and(half == seq, tp == j))
+
+    seed_local = pltpu.make_async_copy(
+        piece_ref, hidden.at[slot, pl.ds(sec * piece, piece), :], h_rsem.at[slot, sec]
+    )
+    for j in range(n_tp):
+        mine = seed_is_mine(j)
+
+        @pl.when(mine)
+        def _():
+            seed_local.start()
+
+        @pl.when(jnp.logical_not(mine))
+        def _():
+            seed_copy(j).start()
+
+    squares = jnp.zeros((tokens, LANES), jnp.float32)
+    for d in range(n_tp):
+        c = (tp + d) % n_tp
+        for k in range(n_sec):
+            pltpu.make_async_copy(
+                hidden.at[c, pl.ds(k * piece, piece), :],
+                hidden.at[c, pl.ds(k * piece, piece), :],
+                h_rsem.at[c, k],
+            ).wait()
+        load_q[d].wait()
+        rows = hidden[c].astype(jnp.float32)
+        sq = rows * rows
+        for k in range(chunk // LANES):
+            squares += sq[:, k * LANES : (k + 1) * LANES]
+        scaled = (rows * gain_ref[pl.ds(c, 1), :]).astype(jnp.bfloat16)
+        if d == n_tp - 1:
+            sq_send[...] = squares
+            sq_copy = pltpu.make_async_remote_copy(
+                src_ref=sq_send,
+                dst_ref=sq_recv,
+                send_sem=q_ssem,
+                recv_sem=q_rsem,
+                device_id={"seq": other},
+                device_id_type=MESH,
+            )
+            sq_copy.start()
+        part_copies = []
+        for g in range(groups):
+            cols = slice(g * group_width, (g + 1) * group_width)
+            product = jnp.dot(
+                scaled,
+                wq[pl.ds(pl.multiple_of(c * chunk, chunk), chunk), cols],
+                preferred_element_type=jnp.float32,
+            )
+            if d > 0:
+                product += acc[:, cols]
+            acc[:, cols] = product
+            if d == n_tp - 1:
+                part_send[g] = product.astype(jnp.bfloat16)
+                copy = pltpu.make_async_remote_copy(
+                    src_ref=part_send.at[g],
+                    dst_ref=part_recv.at[g],
+                    send_sem=p_ssem.at[g],
+                    recv_sem=p_rsem.at[g],
+                    device_id={"seq": other},
+                    device_id_type=MESH,
+                )
+                copy.start()
+                part_copies.append(copy)
+
+    sq_copy.wait_recv()
+    features = n_seq * n_tp * chunk
+    mean = jnp.sum(squares + sq_recv[...], axis=-1, keepdims=True) * (1.0 / features)
+    inverse_rms = lax.rsqrt(mean + EPS)
+    cosine, sine = cos_ref[...], sin_ref[...]
+    ready = []
+    for g in range(groups):
+        part_copies[g].wait_recv()
+        cols = slice(g * group_width, (g + 1) * group_width)
+        whole = (acc[:, cols] + part_recv[g].astype(jnp.float32)) * inverse_rms
+        for k in range(group_width // HEAD_WIDTH):
+            head = whole[:, k * HEAD_WIDTH : (k + 1) * HEAD_WIDTH]
+            if len(ready) < query_heads + kv_heads:
+                head = head * cosine + pltpu.roll(head, HEAD_WIDTH // 2, 1) * sine
+            ready.append(head.astype(jnp.bfloat16))
+
+    repeat = query_heads // kv_heads
+    row_at = lax.broadcasted_iota(jnp.int32, (tokens, tokens), 0)
+    key_at = lax.broadcasted_iota(jnp.int32, (tokens, tokens), 1)
+    visible = key_at <= row_at
+    for h in range(query_heads):
+        keys = ready[query_heads + h // repeat]
+        values = ready[query_heads + kv_heads + h // repeat]
+        scores = lax.dot_general(
+            ready[h], keys, (((1,), (1,)), ((), ())), preferred_element_type=jnp.float32
+        ) * HEAD_WIDTH ** (-0.5)
+        scores = jnp.where(visible, scores, MASKED)
+        shifted = jnp.exp(scores - jnp.max(scores, axis=-1, keepdims=True))
+        weights = (shifted / jnp.sum(shifted, axis=-1, keepdims=True)).astype(jnp.bfloat16)
+        heads[:, h * HEAD_WIDTH : (h + 1) * HEAD_WIDTH] = jnp.dot(
+            weights, values, preferred_element_type=jnp.float32
+        ).astype(jnp.bfloat16)
+
+    load_o.wait()
+    attended = heads[...]
+
+    def rs_copy(d):
+        return pltpu.make_async_remote_copy(
+            src_ref=rs_send.at[d],
+            dst_ref=rs_recv.at[d],
+            send_sem=r_ssem.at[d],
+            recv_sem=r_rsem.at[d],
+            device_id={"tp": (tp + d) % n_tp},
+            device_id_type=MESH,
+        )
+
+    own = None
+    for d in [*range(1, n_tp), 0]:
+        c = (tp + d) % n_tp
+        partial = lax.dot_general(
+            attended,
+            wo[pl.ds(pl.multiple_of(c * chunk, chunk), chunk), :],
+            (((1,), (1,)), ((), ())),
+            preferred_element_type=jnp.float32,
+        ).astype(jnp.bfloat16)
+        if d:
+            rs_send[d] = partial
+            rs_copy(d).start()
+        else:
+            own = partial.astype(jnp.float32)
+    summed = own
+    for d in range(1, n_tp):
+        rs_copy(d).wait_recv()
+        summed += rs_recv[d].astype(jnp.float32)
+    fresh[...] = (hidden[tp].astype(jnp.float32) + summed).astype(jnp.bfloat16)
+
+    def next_copy(j, k):
+        return pltpu.make_async_remote_copy(
+            src_ref=fresh.at[pl.ds(k * piece, piece), :],
+            dst_ref=hidden.at[tp, pl.ds(k * piece, piece), :],
+            send_sem=h_ssem.at[k + 1, j],
+            recv_sem=h_rsem.at[tp, k],
+            device_id={"section": sec + 1, "tp": j},
+            device_id_type=MESH,
+        )
+
+    @pl.when(sec < n_sec - 1)
+    def _():
+        for j in range(n_tp):
+            for k in range(n_sec):
+                next_copy(j, k).start()
+
+    place = seq * n_tp + tp
+    holder, part_of = place // n_seq, place % n_seq
+
+    def out_copy(b):
+        return pltpu.make_async_remote_copy(
+            src_ref=fresh.at[pl.ds(b * block, block), :],
+            dst_ref=out_ref.at[0, :, pl.ds(pl.multiple_of(part_of * chunk, chunk), chunk)],
+            send_sem=o_ssem.at[b],
+            recv_sem=o_rsem.at[part_of],
+            device_id={"seq": b, "tp": holder},
+            device_id_type=MESH,
+        )
+
+    out_local = pltpu.make_async_copy(
+        fresh.at[pl.ds(seq * block, block), :],
+        out_ref.at[0, :, pl.ds(pl.multiple_of(part_of * chunk, chunk), chunk)],
+        o_rsem.at[part_of],
+    )
+    for b in range(n_seq):
+        mine = jnp.logical_and(seq == b, holder == tp)
+
+        @pl.when(mine)
+        def _():
+            out_local.start()
+
+        @pl.when(jnp.logical_not(mine))
+        def _():
+            out_copy(b).start()
+
+    for p in range(n_seq):
+        view = out_ref.at[0, :, pl.ds(p * chunk, chunk)]
+        pltpu.make_async_copy(view, view, o_rsem.at[p]).wait()
+
+    for b in range(n_seq):
+
+        @pl.when(jnp.logical_not(jnp.logical_and(seq == b, holder == tp)))
+        def _():
+            out_copy(b).wait_send()
+
+    @pl.when(sec < n_sec - 1)
+    def _():
+        for j in range(n_tp):
+            for k in range(n_sec):
+                next_copy(j, k).wait_send()
+
+    for d in range(1, n_tp):
+        rs_copy(d).wait_send()
+    for copy in part_copies:
+        copy.wait_send()
+    sq_copy.wait_send()
+    for j in range(n_tp):
+
+        @pl.when(jnp.logical_not(seed_is_mine(j)))
+        def _():
+            seed_copy(j).wait_send()
+
+
+def chained(n_seq, n_sec, n_tp, token_ids, embed_columns, norm_gain, qkv_weight, out_weight):
+    block = token_ids.shape[0]
+    tokens = block * n_seq
+    chunk = embed_columns.shape[0]
+    columns = qkv_weight.shape[2]
+    half = qkv_weight.shape[1]
+    piece = tokens // n_sec
+    groups = 4
+    seq = lax.axis_index("seq")
+    theirs = lax.ppermute(token_ids, "seq", [(0, 1), (1, 0)])
+    every_id = jnp.where(
+        seq == 0,
+        jnp.concatenate([token_ids, theirs]),
+        jnp.concatenate([theirs, token_ids]),
+    )
+    looked = pl.pallas_call(
+        lookup_kernel,
+        out_shape=jax.ShapeDtypeStruct((piece, chunk), jnp.bfloat16),
+        in_specs=[
+            pl.BlockSpec(memory_space=pltpu.SMEM),
+            pl.BlockSpec(memory_space=pltpu.HBM),
+        ],
+        out_specs=pl.BlockSpec(memory_space=pltpu.VMEM),
+        scratch_shapes=[
+            pltpu.VMEM((chunk, piece * LANES), jnp.bfloat16),
+            pltpu.SemaphoreType.DMA((piece,)),
+        ],
+    )(every_id, embed_columns)
+    cosine, sine = rope_tables(jnp.arange(tokens), HEAD_WIDTH)
+    cosine = jnp.concatenate([cosine, cosine], axis=1)
+    sine = jnp.concatenate([-sine, sine], axis=1)
+    gain = lax.dynamic_slice_in_dim(norm_gain[0], seq * half, half).astype(jnp.float32)
+    gain = gain.reshape(n_tp, chunk)
+    vmem = pl.BlockSpec(memory_space=pltpu.VMEM)
+    hbm = pl.BlockSpec(memory_space=pltpu.HBM)
+    dma = pltpu.SemaphoreType.DMA
+    return pl.pallas_call(
+        functools.partial(chain_kernel, n_seq, n_sec, n_tp),
+        out_shape=jax.ShapeDtypeStruct((1, block, n_seq * chunk), jnp.bfloat16),
+        in_specs=[vmem, vmem, vmem, vmem, hbm, hbm],
+        out_specs=vmem,
+        scratch_shapes=[
+            pltpu.VMEM((half, columns), jnp.bfloat16),
+            pltpu.VMEM((half, out_weight.shape[2]), jnp.bfloat16),
+            pltpu.VMEM((n_tp, tokens, chunk), jnp.bfloat16),
+            pltpu.VMEM((tokens, columns), jnp.float32),
+            pltpu.VMEM((groups, tokens, columns // groups), jnp.bfloat16),
+            pltpu.VMEM((groups, tokens, columns // groups), jnp.bfloat16),
+            pltpu.VMEM((tokens, LANES), jnp.float32),
+            pltpu.VMEM((tokens, LANES), jnp.float32),
+            pltpu.VMEM((tokens, out_weight.shape[2]), jnp.bfloat16),
+            pltpu.VMEM((n_tp, tokens, chunk), jnp.bfloat16),
+            pltpu.VMEM((n_tp, tokens, chunk), jnp.bfloat16),
+            pltpu.VMEM((tokens, chunk), jnp.bfloat16),
+            dma((n_tp + 1,)),
+            dma((n_sec + 1, n_tp)),
+            dma((n_tp, n_sec)),
+            dma((groups,)),
+            dma((groups,)),
+            dma,
+            dma,
+            dma((n_tp,)),
+            dma((n_tp,)),
+            dma((n_seq,)),
+            dma((n_seq,)),
+        ],
+        compiler_params=pltpu.CompilerParams(has_side_effects=True),
+    )(looked, gain, cosine, sine, qkv_weight, out_weight)
+
+
 def solution(mesh):
+    counts = tuple(mesh.shape[a] for a in ("seq", "section", "tp"))
+    program = functools.partial(chained, *counts) if counts[0] == 2 else body
     placed = (
         P("seq"),
         P(("tp", "seq"), None),
@@ -162,5 +550,5 @@
         P("section", "seq", "tp"),
     )
     return jax.shard_map(
-        body, mesh=mesh, in_specs=placed, out_specs=P("section", "seq", "tp"), check_vma=False
-    )
+        program, mesh=mesh, in_specs=placed, out_specs=P("section", "seq", "tp"), check_vma=False
+    )

time: 503 us -> 117 us (0.23); the launches traced: 494 us -> 117 us
  waiting for transfers between devices: 251 us -> 0.01 us
  Pallas kernels: 0 us -> 112 us
  local copies, waits for them, and re-layouts: 102 us -> 2.17 us
  blocking collectives: 55.2 us -> 0 us
  matrix products: 51.9 us -> 0 us
  between operations: 14.5 us -> 0.04 us
  other arithmetic: 11.7 us -> 3.12 us
  starting transfers between devices: 7.78 us -> 0.23 us
    pallas_call x0 -> x2, Pallas kernels: none -> 112 us  [the longest x1 106 us: chained(): pl.pallas_call(functools.partial(chain_kernel, n_seq, n_sec, n_tp), out_s...]
    psum x4 -> x0, waiting for transfers between devices: 104 us -> none  [from_root(): return lax.psum(jnp.where(mine, value, jnp.zeros_like(value)), axis)]
    unnamed x10 -> x1, local copies, waits for them, and re-layouts: 87.9 us -> 1.57 us
    reduce_scatter x4 -> x0, waiting for transfers between devices: 76.1 us -> none  [combine(): lax.psum_scatter(partial_value.astype(jnp.bfloat16), 'tp', scatter_dimens...]
    all_gather x2 -> x0, waiting for transfers between devices: 56 us -> none  [the longest x1 55.9 us: body(): lax.all_gather(out_weight, 'seq', axis=1, tiled=True)]
    all_gather x4 -> x0, blocking collectives: 51.5 us -> none  [widen(): return lax.all_gather(current, 'tp', axis=1, tiled=True)]
    dot_general x12 -> x0, matrix products: 47.2 us -> none  [the longest x4 24.2 us: project(): jnp.dot(normed, qkv_full, preferred_element_type=jnp.float32)]
    dot_general x1 -> x0, local copies, waits for them, and re-layouts: 11.3 us -> none  [project(): jnp.dot(normed, qkv_full, preferred_element_type=jnp.float32)]
  transfers between devices with their start and end apart: 14 -> 1, of which waited for: 13 -> 0; matrix products, arithmetic and copies ran while one was open for 19% -> 2% of each run, Pallas kernels for 0% -> 0%
where the time goes in v1:
time: 117 us
  Pallas kernels  112 us (96%)
  other arithmetic  3.12 us (3%)
  local copies, waits for them, and re-layouts  2.17 us (2%)
    pallas_call x1, Pallas kernels, chained(): pl.pallas_call(functools.partial(chain_kernel, n_seq, n_sec, n_tp), out_s...  106 us
    pallas_call x1, Pallas kernels, chained(): pl.pallas_call(lookup_kernel, out_shape=jax.ShapeDtypeStruct((piece, chun...  5.88 us
  transfers between devices with their start and end apart: 1, of which 0 were waited for; matrix products, arithmetic and copies ran while one was open for 2% of the time, Pallas kernels for 0%

profile of v1, /device:TPU:15, one launch (start us, length us, event | category | flops | bytes accessed | tf_op | source)
XLA Modules:
  0.0 117.1 jit_solution(9227929471289749302)
XLA Ops:
  0.0 0.2 collective-permute-start
  0.2 0.3 fusion
  0.6 0.8 pad_maximum_fusion
  1.3 0.7 convert_reduce_fusion
  2.0 0.6 reshape.16.gain_ref
  2.7 0.0 collective-permute-done
  2.7 1.3 %broadcast_select_fusion.ids_ref = s32[128]{0:T(128)} fusion(pred[]{:T(512)S(6)} %eq.3, s32[64]{0:T(128)S(1)} %collective-permute-done, s32[64]{0:T(128)} %param.5), kind=kLoop, calls=%fused_computation.6 | loop fusion | flops 384 | bytes 1025 | tf_op jit(solution)/shard_map/jit(_where)/select_n | solution.py:482
  4.0 5.9 %shard_map.55.piece_ref = bf16[32,512]{1,0:T(8,128)(2,1)} custom-call(s32[128]{0:T(128)} %broadcast_select_fusion.ids_ref, bf16[512,65536]{1,0:T(8,128)(2,1)} %table_ref.1), custom_call_target="tpu_custom_call" | custom-call | tf_op jit(solution)/shard_map/pallas_call | solution.py:487
  9.9 105.7 %shard_map.56 = bf16[1,64,1024]{2,1,0:T(8,128)(2,1)} custom-call(bf16[32,512]{1,0:T(8,128)(2,1)} %shard_map.55.piece_ref, f32[4,512]{1,0:T(4,128)} %reshape.16.gain_ref, f32[128,128]{1,0:T(8,128)} %get-tuple-element.8.cos_ref, f32[128,128]{1,0:T(8,128)} %get-tuple-element.9.sin_ref, bf16[1,2048,1024]{2,1,0:T(8,128)(2,1)} %qkv_ref.1, ...), custom_call_target="tpu_custom_call" | custom-call | tf_op jit(solution)/shard_map/pallas_call | solution.py:508
  115.5 1.6 %copy.7 = bf16[1,64,1024]{2,1,0:T(8,128)(2,1)} copy(bf16[1,64,1024]{2,1,0:T(8,128)(2,1)} %shard_map.56) | data formatting | bytes 262144
  (2 shorter events, 0.0 us)
Async XLA Ops:
  0.0 2.7 %collective-permute-start = (s32[64]{0:T(128)}, s32[64]{0:T(128)S(1)}, u32[]{:S(2)}, u32[]{:S(2)}) collective-permute-start(s32[64]{0:T(128)} %param.5), channel_id=1, source_target_pairs={{0,16},{16,0},{1,17},{17,1},{2,18},{18,2},{3,19},{19,3},{4,20},{20... | collective-permute-start | bytes 776 | tf_op jit(solution)/shard_map/ppermute | solution.py:481

commit v2 on v1

--- a/solution.py
+++ b/solution.py
@@ -162,13 +162,19 @@
 MESH = pl.DeviceIdType.MESH
 
 
-def lookup_kernel(ids_ref, table_ref, out_ref, tiles, sems):
+def lookup_kernel(mine_ref, theirs_ref, table_ref, out_ref, tiles, sems):
     count = out_ref.shape[0]
     width = table_ref.shape[0]
+    block = mine_ref.shape[0]
     first = lax.axis_index("section") * count
+    ours = first // block == lax.axis_index("seq")
+    ids = [
+        jnp.where(ours, mine_ref[first % block + i], theirs_ref[first % block + i])
+        for i in range(count)
+    ]
 
     def fetch(i):
-        start = pl.multiple_of((ids_ref[first + i] // LANES) * LANES, LANES)
+        start = pl.multiple_of((ids[i] // LANES) * LANES, LANES)
         return pltpu.make_async_copy(
             table_ref.at[:, pl.ds(start, LANES)], tiles.at[:, pl.ds(i * LANES, LANES)], sems.at[i]
         )
@@ -182,7 +188,7 @@
     for base in range(0, count, group):
         picks = []
         for i in range(base, base + group):
-            chosen = jnp.logical_and(rows == ids_ref[first + i] % LANES, columns == i)
+            chosen = jnp.logical_and(rows == ids[i] % LANES, columns == i)
             picks.append(jnp.where(chosen, 1.0, 0.0).astype(jnp.bfloat16))
         pick = jnp.concatenate(picks, axis=0)
         for i in range(base, base + group):
@@ -212,6 +218,7 @@
     part_recv,
     sq_send,
     sq_recv,
+    kept,
     heads,
     rs_send,
     rs_recv,
@@ -229,11 +236,10 @@
     o_rsem,
 ):
     seq, sec, tp = (lax.axis_index(a) for a in ("seq", "section", "tp"))
-    other = 1 - seq
     tokens, chunk = fresh.shape
     piece = tokens // n_sec
     block = out_ref.shape[1]
-    groups, _, group_width = part_send.shape
+    _, groups, _, group_width = part_send.shape
     query_heads = QUERY_HEADS // n_tp
     kv_heads = KEY_VALUE_HEADS // n_tp
 
@@ -280,137 +286,48 @@
         def _():
             seed_copy(j).start()
 
-    squares = jnp.zeros((tokens, LANES), jnp.float32)
-    for d in range(n_tp):
-        c = (tp + d) % n_tp
-        for k in range(n_sec):
-            pltpu.make_async_copy(
-                hidden.at[c, pl.ds(k * piece, piece), :],
-                hidden.at[c, pl.ds(k * piece, piece), :],
-                h_rsem.at[c, k],
-            ).wait()
-        load_q[d].wait()
-        rows = hidden[c].astype(jnp.float32)
-        sq = rows * rows
-        for k in range(chunk // LANES):
-            squares += sq[:, k * LANES : (k + 1) * LANES]
-        scaled = (rows * gain_ref[pl.ds(c, 1), :]).astype(jnp.bfloat16)
-        if d == n_tp - 1:
-            sq_send[...] = squares
-            sq_copy = pltpu.make_async_remote_copy(
-                src_ref=sq_send,
-                dst_ref=sq_recv,
-                send_sem=q_ssem,
-                recv_sem=q_rsem,
-                device_id={"seq": other},
-                device_id_type=MESH,
-            )
-            sq_copy.start()
-        part_copies = []
-        for g in range(groups):
-            cols = slice(g * group_width, (g + 1) * group_width)
-            product = jnp.dot(
-                scaled,
-                wq[pl.ds(pl.multiple_of(c * chunk, chunk), chunk), cols],
-                preferred_element_type=jnp.float32,
-            )
-            if d > 0:
-                product += acc[:, cols]
-            acc[:, cols] = product
-            if d == n_tp - 1:
-                part_send[g] = product.astype(jnp.bfloat16)
-                copy = pltpu.make_async_remote_copy(
-                    src_ref=part_send.at[g],
-                    dst_ref=part_recv.at[g],
-                    send_sem=p_ssem.at[g],
-                    recv_sem=p_rsem.at[g],
-                    device_id={"seq": other},
-                    device_id_type=MESH,
-                )
-                copy.start()
-                part_copies.append(copy)
-
-    sq_copy.wait_recv()
-    features = n_seq * n_tp * chunk
-    mean = jnp.sum(squares + sq_recv[...], axis=-1, keepdims=True) * (1.0 / features)
-    inverse_rms = lax.rsqrt(mean + EPS)
-    cosine, sine = cos_ref[...], sin_ref[...]
-    ready = []
-    for g in range(groups):
-        part_copies[g].wait_recv()
-        cols = slice(g * group_width, (g + 1) * group_width)
-        whole = (acc[:, cols] + part_recv[g].astype(jnp.float32)) * inverse_rms
-        for k in range(group_width // HEAD_WIDTH):
-            head = whole[:, k * HEAD_WIDTH : (k + 1) * HEAD_WIDTH]
-            if len(ready) < query_heads + kv_heads:
-                head = head * cosine + pltpu.roll(head, HEAD_WIDTH // 2, 1) * sine
-            ready.append(head.astype(jnp.bfloat16))
-
-    repeat = query_heads // kv_heads
-    row_at = lax.broadcasted_iota(jnp.int32, (tokens, tokens), 0)
-    key_at = lax.broadcasted_iota(jnp.int32, (tokens, tokens), 1)
-    visible = key_at <= row_at
-    for h in range(query_heads):
-        keys = ready[query_heads + h // repeat]
-        values = ready[query_heads + kv_heads + h // repeat]
-        scores = lax.dot_general(
-            ready[h], keys, (((1,), (1,)), ((), ())), preferred_element_type=jnp.float32
-        ) * HEAD_WIDTH ** (-0.5)
-        scores = jnp.where(visible, scores, MASKED)
-        shifted = jnp.exp(scores - jnp.max(scores, axis=-1, keepdims=True))
-        weights = (shifted / jnp.sum(shifted, axis=-1, keepdims=True)).astype(jnp.bfloat16)
-        heads[:, h * HEAD_WIDTH : (h + 1) * HEAD_WIDTH] = jnp.dot(
-            weights, values, preferred_element_type=jnp.float32
-        ).astype(jnp.bfloat16)
-
-    load_o.wait()
-    attended = heads[...]
-
-    def rs_copy(d):
+    other = 1 - seq
+    pieces = block // piece
+
+    def square_copy(p):
         return pltpu.make_async_remote_copy(
-            src_ref=rs_send.at[d],
-            dst_ref=rs_recv.at[d],
-            send_sem=r_ssem.at[d],
-            recv_sem=r_rsem.at[d],
+            src_ref=sq_send.at[p],
+            dst_ref=sq_recv.at[p],
+            send_sem=q_ssem.at[p],
+            recv_sem=q_rsem.at[p],
+            device_id={"seq": other},
+            device_id_type=MESH,
+        )
+
+    def part_copy(p, g):
+        return pltpu.make_async_remote_copy(
+            src_ref=part_send.at[p, g],
+            dst_ref=part_recv.at[p, g],
+            send_sem=p_ssem.at[p, g],
+            recv_sem=p_rsem.at[p, g],
+            device_id={"seq": other},
+            device_id_type=MESH,
+        )
+
+    def rs_copy(p, d):
+        return pltpu.make_async_remote_copy(
+            src_ref=rs_send.at[p, d],
+            dst_ref=rs_recv.at[p, d],
+            send_sem=r_ssem.at[p, d],
+            recv_sem=r_rsem.at[p, d],
             device_id={"tp": (tp + d) % n_tp},
             device_id_type=MESH,
         )
 
-    own = None
-    for d in [*range(1, n_tp), 0]:
-        c = (tp + d) % n_tp
-        partial = lax.dot_general(
-            attended,
-            wo[pl.ds(pl.multiple_of(c * chunk, chunk), chunk), :],
-            (((1,), (1,)), ((), ())),
-            preferred_element_type=jnp.float32,
-        ).astype(jnp.bfloat16)
-        if d:
-            rs_send[d] = partial
-            rs_copy(d).start()
-        else:
-            own = partial.astype(jnp.float32)
-    summed = own
-    for d in range(1, n_tp):
-        rs_copy(d).wait_recv()
-        summed += rs_recv[d].astype(jnp.float32)
-    fresh[...] = (hidden[tp].astype(jnp.float32) + summed).astype(jnp.bfloat16)
-
-    def next_copy(j, k):
+    def next_copy(d, k):
         return pltpu.make_async_remote_copy(
             src_ref=fresh.at[pl.ds(k * piece, piece), :],
             dst_ref=hidden.at[tp, pl.ds(k * piece, piece), :],
-            send_sem=h_ssem.at[k + 1, j],
+            send_sem=h_ssem.at[k + 1, d],
             recv_sem=h_rsem.at[tp, k],
-            device_id={"section": sec + 1, "tp": j},
+            device_id={"section": sec + 1, "tp": (tp + n_tp - d) % n_tp},
             device_id_type=MESH,
         )
-
-    @pl.when(sec < n_sec - 1)
-    def _():
-        for j in range(n_tp):
-            for k in range(n_sec):
-                next_copy(j, k).start()
 
     place = seq * n_tp + tp
     holder, part_of = place // n_seq, place % n_seq
@@ -425,43 +342,152 @@
             device_id_type=MESH,
         )
 
-    out_local = pltpu.make_async_copy(
-        fresh.at[pl.ds(seq * block, block), :],
-        out_ref.at[0, :, pl.ds(pl.multiple_of(part_of * chunk, chunk), chunk)],
-        o_rsem.at[part_of],
-    )
-    for b in range(n_seq):
-        mine = jnp.logical_and(seq == b, holder == tp)
+    def project(p):
+        span = slice(p * block, (p + 1) * block)
+        squares = jnp.zeros((block, LANES), jnp.float32)
+        for d in range(n_tp):
+            c = (tp + d) % n_tp
+            for k in range(p * pieces, (p + 1) * pieces):
+                view = hidden.at[c, pl.ds(k * piece, piece), :]
+                pltpu.make_async_copy(view, view, h_rsem.at[c, k]).wait()
+            if p == 0:
+                load_q[d].wait()
+            rows = hidden[c, span, :].astype(jnp.float32)
+            sq = rows * rows
+            for k in range(chunk // LANES):
+                squares += sq[:, k * LANES : (k + 1) * LANES]
+            at = pl.multiple_of(seq * (n_tp * chunk) + c * chunk, chunk)
+            gain = gain_ref[:, pl.ds(at, chunk)].astype(jnp.float32)
+            scaled = (rows * gain).astype(jnp.bfloat16)
+            if d == n_tp - 1:
+                sq_send[p] = squares
+                square_copy(p).start()
+            for g in range(groups):
+                cols = slice(g * group_width, (g + 1) * group_width)
+                product = jnp.dot(
+                    scaled,
+                    wq[pl.ds(pl.multiple_of(c * chunk, chunk), chunk), cols],
+                    preferred_element_type=jnp.float32,
+                )
+                if d > 0:
+                    product += acc[span, cols]
+                acc[span, cols] = product
+                if d == n_tp - 1:
+                    part_send[p, g] = product.astype(jnp.bfloat16)
+                    part_copy(p, g).start()
+
+    repeat = query_heads // kv_heads
+
+    def attend_block(p):
+        span = slice(p * block, (p + 1) * block)
+        square_copy(p).wait_recv()
+        features = n_seq * n_tp * chunk
+        mean = jnp.sum(sq_send[p] + sq_recv[p], axis=-1, keepdims=True) * (1.0 / features)
+        inverse_rms = lax.rsqrt(mean + EPS)
+        cosine, sine = cos_ref[span, :], sin_ref[span, :]
+        ready = []
+        for g in range(groups):
+            part_copy(p, g).wait_recv()
+            cols = slice(g * group_width, (g + 1) * group_width)
+            whole = (acc[span, cols] + part_recv[p, g].astype(jnp.float32)) * inverse_rms
+            for k in range(group_width // HEAD_WIDTH):
+                head = whole[:, k * HEAD_WIDTH : (k + 1) * HEAD_WIDTH]
+                if len(ready) < query_heads + kv_heads:
+                    head = head * cosine + pltpu.roll(head, HEAD_WIDTH // 2, 1) * sine
+                head = head.astype(jnp.bfloat16)
+                if len(ready) >= query_heads:
+                    kept[len(ready) - query_heads, span, :] = head
+                ready.append(head)
+        known = (p + 1) * block
+        row_at = lax.broadcasted_iota(jnp.int32, (repeat, block, known), 1)
+        key_at = lax.broadcasted_iota(jnp.int32, (repeat, block, known), 2)
+        visible = (key_at <= row_at + p * block).reshape(repeat * block, known)
+        for h in range(kv_heads):
+            queries = jnp.concatenate(ready[h * repeat : (h + 1) * repeat], axis=0)
+            scores = lax.dot_general(
+                queries, kept[h, :known, :], (((1,), (1,)), ((), ())), preferred_element_type=jnp.float32
+            ) * HEAD_WIDTH ** (-0.5)
+            scores = jnp.where(visible, scores, MASKED)
+            shifted = jnp.exp(scores - jnp.max(scores, axis=-1, keepdims=True))
+            weights = (shifted / jnp.sum(shifted, axis=-1, keepdims=True)).astype(jnp.bfloat16)
+            attended = jnp.dot(
+                weights, kept[kv_heads + h, :known, :], preferred_element_type=jnp.float32
+            ).astype(jnp.bfloat16)
+            for r in range(repeat):
+                at = (h * repeat + r) * HEAD_WIDTH
+                heads[span, at : at + HEAD_WIDTH] = attended[r * block : (r + 1) * block]
+        if p == 0:
+            load_o.wait()
+        attended = heads[span, :]
+        for d in [*range(1, n_tp), 0]:
+            c = (tp + d) % n_tp
+            partial = lax.dot_general(
+                attended,
+                wo[pl.ds(pl.multiple_of(c * chunk, chunk), chunk), :],
+                (((1,), (1,)), ((), ())),
+                preferred_element_type=jnp.float32,
+            ).astype(jnp.bfloat16)
+            rs_send[p, d] = partial
+            if d:
+                rs_copy(p, d).start()
+
+    def forward(p):
+        span = slice(p * block, (p + 1) * block)
+        summed = rs_send[p, 0].astype(jnp.float32)
+        for d in range(1, n_tp):
+            rs_copy(p, d).wait_recv()
+            summed += rs_recv[p, d].astype(jnp.float32)
+        fresh[span, :] = (hidden[tp, span, :].astype(jnp.float32) + summed).astype(jnp.bfloat16)
+
+        @pl.when(sec < n_sec - 1)
+        def _():
+            for d in range(n_tp):
+                for k in range(p * pieces, (p + 1) * pieces):
+                    next_copy(d, k).start()
+
+        mine = jnp.logical_and(seq == p, holder == tp)
 
         @pl.when(mine)
         def _():
-            out_local.start()
+            pltpu.make_async_copy(
+                fresh.at[pl.ds(seq * block, block), :],
+                out_ref.at[0, :, pl.ds(pl.multiple_of(part_of * chunk, chunk), chunk)],
+                o_rsem.at[part_of],
+            ).start()
 
         @pl.when(jnp.logical_not(mine))
         def _():
-            out_copy(b).start()
+            out_copy(p).start()
+
+    project(0)
+    attend_block(0)
+    project(1)
+    forward(0)
+    attend_block(1)
+    forward(1)
 
     for p in range(n_seq):
         view = out_ref.at[0, :, pl.ds(p * chunk, chunk)]
         pltpu.make_async_copy(view, view, o_rsem.at[p]).wait()
 
-    for b in range(n_seq):
-
-        @pl.when(jnp.logical_not(jnp.logical_and(seq == b, holder == tp)))
-        def _():
-            out_copy(b).wait_send()
+    for p in range(n_seq):
+
+        @pl.when(jnp.logical_not(jnp.logical_and(seq == p, holder == tp)))
+        def _():
+            out_copy(p).wait_send()
 
     @pl.when(sec < n_sec - 1)
     def _():
-        for j in range(n_tp):
+        for d in range(n_tp):
             for k in range(n_sec):
-                next_copy(j, k).wait_send()
-
-    for d in range(1, n_tp):
-        rs_copy(d).wait_send()
-    for copy in part_copies:
-        copy.wait_send()
-    sq_copy.wait_send()
+                next_copy(d, k).wait_send()
+
+    for p in range(n_seq):
+        for d in range(1, n_tp):
+            rs_copy(p, d).wait_send()
+        for g in range(groups):
+            part_copy(p, g).wait_send()
+        square_copy(p).wait_send()
     for j in range(n_tp):
 
         @pl.when(jnp.logical_not(seed_is_mine(j)))
@@ -477,17 +503,12 @@
     half = qkv_weight.shape[1]
     piece = tokens // n_sec
     groups = 4
-    seq = lax.axis_index("seq")
     theirs = lax.ppermute(token_ids, "seq", [(0, 1), (1, 0)])
-    every_id = jnp.where(
-        seq == 0,
-        jnp.concatenate([token_ids, theirs]),
-        jnp.concatenate([theirs, token_ids]),
-    )
     looked = pl.pallas_call(
         lookup_kernel,
         out_shape=jax.ShapeDtypeStruct((piece, chunk), jnp.bfloat16),
         in_specs=[
+            pl.BlockSpec(memory_space=pltpu.SMEM),
             pl.BlockSpec(memory_space=pltpu.SMEM),
             pl.BlockSpec(memory_space=pltpu.HBM),
         ],
@@ -496,12 +517,10 @@
             pltpu.VMEM((chunk, piece * LANES), jnp.bfloat16),
             pltpu.SemaphoreType.DMA((piece,)),
         ],
-    )(every_id, embed_columns)
+    )(token_ids, theirs, embed_columns)
     cosine, sine = rope_tables(jnp.arange(tokens), HEAD_WIDTH)
     cosine = jnp.concatenate([cosine, cosine], axis=1)
     sine = jnp.concatenate([-sine, sine], axis=1)
-    gain = lax.dynamic_slice_in_dim(norm_gain[0], seq * half, half).astype(jnp.float32)
-    gain = gain.reshape(n_tp, chunk)
     vmem = pl.BlockSpec(memory_space=pltpu.VMEM)
     hbm = pl.BlockSpec(memory_space=pltpu.HBM)
     dma = pltpu.SemaphoreType.DMA
@@ -515,28 +534,29 @@
             pltpu.VMEM((half, out_weight.shape[2]), jnp.bfloat16),
             pltpu.VMEM((n_tp, tokens, chunk), jnp.bfloat16),
             pltpu.VMEM((tokens, columns), jnp.float32),
-            pltpu.VMEM((groups, tokens, columns // groups), jnp.bfloat16),
-            pltpu.VMEM((groups, tokens, columns // groups), jnp.bfloat16),
-            pltpu.VMEM((tokens, LANES), jnp.float32),
-            pltpu.VMEM((tokens, LANES), jnp.float32),
+            pltpu.VMEM((n_seq, groups, block, columns // groups), jnp.bfloat16),
+            pltpu.VMEM((n_seq, groups, block, columns // groups), jnp.bfloat16),
+            pltpu.VMEM((n_seq, block, LANES), jnp.float32),
+            pltpu.VMEM((n_seq, block, LANES), jnp.float32),
+            pltpu.VMEM((2 * KEY_VALUE_HEADS // n_tp, tokens, HEAD_WIDTH), jnp.bfloat16),
             pltpu.VMEM((tokens, out_weight.shape[2]), jnp.bfloat16),
-            pltpu.VMEM((n_tp, tokens, chunk), jnp.bfloat16),
-            pltpu.VMEM((n_tp, tokens, chunk), jnp.bfloat16),
+            pltpu.VMEM((n_seq, n_tp, block, chunk), jnp.bfloat16),
+            pltpu.VMEM((n_seq, n_tp, block, chunk), jnp.bfloat16),
             pltpu.VMEM((tokens, chunk), jnp.bfloat16),
             dma((n_tp + 1,)),
             dma((n_sec + 1, n_tp)),
             dma((n_tp, n_sec)),
-            dma((groups,)),
-            dma((groups,)),
-            dma,
-            dma,
-            dma((n_tp,)),
-            dma((n_tp,)),
+            dma((n_seq, groups)),
+            dma((n_seq, groups)),
+            dma((n_seq,)),
+            dma((n_seq,)),
+            dma((n_seq, n_tp)),
+            dma((n_seq, n_tp)),
             dma((n_seq,)),
             dma((n_seq,)),
         ],
         compiler_params=pltpu.CompilerParams(has_side_effects=True),
-    )(looked, gain, cosine, sine, qkv_weight, out_weight)
+    )(looked, norm_gain, cosine, sine, qkv_weight, out_weight)
 
 
 def solution(mesh):

time: 117 us -> 98.7 us (0.84)
  Pallas kernels: 112 us -> 93.8 us
  other arithmetic: 3.12 us -> 1.07 us
  waiting for transfers between devices: 0.01 us -> 1.25 us
    pallas_call x1, Pallas kernels: 106 us -> 88 us  [chained(): pl.pallas_call(functools.partial(chain_kernel, n_seq, n_sec, n_tp), out_s...]
    select_n x1 -> x0, other arithmetic: 1.31 us -> none  [chained(): jnp.where(seq == 0, jnp.concatenate([token_ids, theirs]), jnp.concatenate...]
    ppermute x1, waiting for transfers between devices: 0.01 us -> 1.25 us  [chained(): theirs = lax.ppermute(token_ids, 'seq', [(0, 1), (1, 0)])]
  transfers between devices with their start and end apart: 1 -> 1, of which waited for: 0 -> 1; matrix products, arithmetic and copies ran while one was open for 2% -> 1% of each run, Pallas kernels for 0% -> 0%
where the time goes in v2:
time: 98.7 us; the launch traced here: 98.5 us
  Pallas kernels  93.8 us (95%)
  local copies, waits for them, and re-layouts  2.11 us (2%)
  waiting for transfers between devices  1.25 us (1%)
  other arithmetic  1.07 us (1%)
    pallas_call x1, Pallas kernels, chained(): pl.pallas_call(functools.partial(chain_kernel, n_seq, n_sec, n_tp), out_s...  88 us
    pallas_call x1, Pallas kernels, chained(): pl.pallas_call(lookup_kernel, out_shape=jax.ShapeDtypeStruct((piece, chun...  5.85 us
    unnamed x3, local copies, waits for them, and re-layouts  2.11 us
  transfers between devices with their start and end apart: 1, of which 1 were waited for; matrix products, arithmetic and copies ran while one was open for 1% of the time, Pallas kernels for 0%

profile of v2, /device:TPU:15, one launch (start us, length us, event | category | flops | bytes accessed | tf_op | source)
XLA Modules:
  0.0 98.5 jit_solution(7195839734683398365)
XLA Ops:
  0.0 0.2 collective-permute-start
  0.2 0.3 fusion
  0.6 0.7 pad_maximum_fusion
  1.3 1.2 %collective-permute-done.theirs_ref = s32[64]{0:T(128)S(1)} collective-permute-done((s32[64]{0:T(128)}, s32[64]{0:T(128)S(1)}, u32[]{:S(2)}, u32[]{:S(2)}) %collective-permute-start) | collective-permute-done | bytes 288 | tf_op jit(solution)/shard_map/ppermute | solution.py:506
  2.6 0.0 copy-start
  2.6 0.5 copy-done
  3.1 5.8 %shard_map.55.piece_ref = bf16[32,512]{1,0:T(8,128)(2,1)} custom-call(s32[64]{0:T(128)} %mine_ref.1, s32[64]{0:T(128)} %copy-done, bf16[512,65536]{1,0:T(8,128)(2,1)} %table_ref.1), custom_call_target="tpu_custom_call" | custom-call | tf_op jit(solution)/shard_map/pallas_call | solution.py:507
  9.0 88.0 %shard_map.56 = bf16[1,64,1024]{2,1,0:T(8,128)(2,1)} custom-call(bf16[32,512]{1,0:T(8,128)(2,1)} %shard_map.55.piece_ref, bf16[1,4096]{1,0:T(2,128)(2,1)} %gain_ref.1, f32[128,128]{1,0:T(8,128)} %get-tuple-element.8.cos_ref, f32[128,128]{1,0:T(8,128)} %get-tuple-element.9.sin_ref, bf16[1,2048,1024]{2,1,0:T(8,128)(2,1)} %qkv_ref.1, bf16[1,2048,512]{2,1,0:T(8,128)(2,1)} %outw_ref.1), custom_call_target="tpu_custom_call" | custom-call | tf_op jit(solution)/shard_map/pallas_call | solution.py:527
  96.9 1.6 %copy.7 = bf16[1,64,1024]{2,1,0:T(8,128)(2,1)} copy(bf16[1,64,1024]{2,1,0:T(8,128)(2,1)} %shard_map.56) | data formatting | bytes 262144
  (2 shorter events, 0.0 us)
Async XLA Ops:
  0.0 2.6 %collective-permute-start = (s32[64]{0:T(128)}, s32[64]{0:T(128)S(1)}, u32[]{:S(2)}, u32[]{:S(2)}) collective-permute-start(s32[64]{0:T(128)} %mine_ref.1), channel_id=1, source_target_pairs={{0,16},{16,0},{1,17},{17,1},{2,18},{18,2},{3,19},{19,3},{4,20},{20... | collective-permute-start | bytes 776 | tf_op jit(solution)/shard_map/ppermute | solution.py:506
  2.6 0.5 copy-start

commit v3 on v2

--- a/solution.py
+++ b/solution.py
@@ -223,6 +223,9 @@
     rs_send,
     rs_recv,
     fresh,
+    relay,
+    a_ssem,
+    a_rsem,
     w_sem,
     h_ssem,
     h_rsem,
@@ -256,35 +259,48 @@
         c.start()
     load_o.start()
 
-    shard = tp * n_seq + seq
-    half, slot = shard // n_tp, shard % n_tp
-
-    def seed_copy(j):
+    def spread_copy(d):
         return pltpu.make_async_remote_copy(
             src_ref=piece_ref,
-            dst_ref=hidden.at[slot, pl.ds(sec * piece, piece), :],
-            send_sem=h_ssem.at[0, j],
+            dst_ref=relay.at[tp],
+            send_sem=a_ssem.at[d],
+            recv_sem=a_rsem.at[tp],
+            device_id={"tp": (tp + d) % n_tp},
+            device_id_type=MESH,
+        )
+
+    def seed(d):
+        source = (tp + n_tp - d) % n_tp
+        shard = source * n_seq + seq
+        half, slot = shard // n_tp, shard % n_tp
+        held = relay.at[source] if d else piece_ref
+        target = hidden.at[slot, pl.ds(sec * piece, piece), :]
+        mine = jnp.logical_and(sec == 0, half == seq)
+        local = pltpu.make_async_copy(held, target, h_rsem.at[slot, sec])
+        remote = pltpu.make_async_remote_copy(
+            src_ref=held,
+            dst_ref=target,
+            send_sem=h_ssem.at[0, d],
             recv_sem=h_rsem.at[slot, sec],
-            device_id={"seq": half, "section": 0, "tp": j},
-            device_id_type=MESH,
-        )
-
-    def seed_is_mine(j):
-        return jnp.logical_and(sec == 0, jnp.logical_and(half == seq, tp == j))
-
-    seed_local = pltpu.make_async_copy(
-        piece_ref, hidden.at[slot, pl.ds(sec * piece, piece), :], h_rsem.at[slot, sec]
-    )
-    for j in range(n_tp):
-        mine = seed_is_mine(j)
+            device_id={"seq": half, "section": 0},
+            device_id_type=MESH,
+        )
+        return source, mine, local, remote
+
+    for d in range(1, n_tp):
+        spread_copy(d).start()
+    for d in range(n_tp):
+        source, mine, local, remote = seed(d)
+        if d:
+            pltpu.make_async_copy(relay.at[source], relay.at[source], a_rsem.at[source]).wait()
 
         @pl.when(mine)
         def _():
-            seed_local.start()
+            local.start()
 
         @pl.when(jnp.logical_not(mine))
         def _():
-            seed_copy(j).start()
+            remote.start()
 
     other = 1 - seq
     pieces = block // piece
@@ -488,11 +504,15 @@
         for g in range(groups):
             part_copy(p, g).wait_send()
         square_copy(p).wait_send()
-    for j in range(n_tp):
-
-        @pl.when(jnp.logical_not(seed_is_mine(j)))
-        def _():
-            seed_copy(j).wait_send()
+    for d in range(n_tp):
+        _, mine, _, remote = seed(d)
+
+        @pl.when(jnp.logical_not(mine))
+        def _():
+            remote.wait_send()
+
+        if d:
+            spread_copy(d).wait_send()
 
 
 def chained(n_seq, n_sec, n_tp, token_ids, embed_columns, norm_gain, qkv_weight, out_weight):
@@ -543,6 +563,9 @@
             pltpu.VMEM((n_seq, n_tp, block, chunk), jnp.bfloat16),
             pltpu.VMEM((n_seq, n_tp, block, chunk), jnp.bfloat16),
             pltpu.VMEM((tokens, chunk), jnp.bfloat16),
+            pltpu.VMEM((n_tp, piece, chunk), jnp.bfloat16),
+            dma((n_tp,)),
+            dma((n_tp,)),
             dma((n_tp + 1,)),
             dma((n_sec + 1, n_tp)),
             dma((n_tp, n_sec)),

time: 98.7 us -> 101 us (1.023)
  Pallas kernels: 93.8 us -> 96.5 us
    pallas_call x1, Pallas kernels: 88 us -> 90.6 us  [chained(): pl.pallas_call(functools.partial(chain_kernel, n_seq, n_sec, n_tp), out_s...]
where the time goes in v3:
time: 101 us
  Pallas kernels  96.5 us (96%)
  local copies, waits for them, and re-layouts  2.11 us (2%)
  waiting for transfers between devices  1.25 us (1%)
  other arithmetic  1.07 us (1%)
    pallas_call x1, Pallas kernels, chained(): pl.pallas_call(functools.partial(chain_kernel, n_seq, n_sec, n_tp), out_s...  90.6 us
    pallas_call x1, Pallas kernels, chained(): pl.pallas_call(lookup_kernel, out_shape=jax.ShapeDtypeStruct((piece, chun...  5.85 us
    unnamed x3, local copies, waits for them, and re-layouts  2.11 us
  transfers between devices with their start and end apart: 1, of which 1 were waited for; matrix products, arithmetic and copies ran while one was open for 1% of the time, Pallas kernels for 0%

profile of v3, /device:TPU:15, one launch (start us, length us, event | category | flops | bytes accessed | tf_op | source)
XLA Modules:
  0.0 101.1 jit_solution(15084046976852916042)
XLA Ops:
  0.0 0.2 collective-permute-start
  0.2 0.3 fusion
  0.6 0.7 pad_maximum_fusion
  1.3 1.2 %collective-permute-done.theirs_ref = s32[64]{0:T(128)S(1)} collective-permute-done((s32[64]{0:T(128)}, s32[64]{0:T(128)S(1)}, u32[]{:S(2)}, u32[]{:S(2)}) %collective-permute-start) | collective-permute-done | bytes 288 | tf_op jit(solution)/shard_map/ppermute | solution.py:526
  2.6 0.0 copy-start
  2.6 0.5 copy-done
  3.1 5.8 %shard_map.55.piece_ref = bf16[32,512]{1,0:T(8,128)(2,1)} custom-call(s32[64]{0:T(128)} %mine_ref.1, s32[64]{0:T(128)} %copy-done, bf16[512,65536]{1,0:T(8,128)(2,1)} %table_ref.1), custom_call_target="tpu_custom_call" | custom-call | tf_op jit(solution)/shard_map/pallas_call | solution.py:527
  9.0 90.6 %shard_map.56 = bf16[1,64,1024]{2,1,0:T(8,128)(2,1)} custom-call(bf16[32,512]{1,0:T(8,128)(2,1)} %shard_map.55.piece_ref, bf16[1,4096]{1,0:T(2,128)(2,1)} %gain_ref.1, f32[128,128]{1,0:T(8,128)} %get-tuple-element.8.cos_ref, f32[128,128]{1,0:T(8,128)} %get-tuple-element.9.sin_ref, bf16[1,2048,1024]{2,1,0:T(8,128)(2,1)} %qkv_ref.1, bf16[1,2048,512]{2,1,0:T(8,128)(2,1)} %outw_ref.1), custom_call_target="tpu_custom_call" | custom-call | tf_op jit(solution)/shard_map/pallas_call | solution.py:547
  99.6 1.6 %copy.7 = bf16[1,64,1024]{2,1,0:T(8,128)(2,1)} copy(bf16[1,64,1024]{2,1,0:T(8,128)(2,1)} %shard_map.56) | data formatting | bytes 262144
  (2 shorter events, 0.0 us)
Async XLA Ops:
  0.0 2.6 %collective-permute-start = (s32[64]{0:T(128)}, s32[64]{0:T(128)S(1)}, u32[]{:S(2)}, u32[]{:S(2)}) collective-permute-start(s32[64]{0:T(128)} %mine_ref.1), channel_id=1, source_target_pairs={{0,16},{16,0},{1,17},{17,1},{2,18},{18,2},{3,19},{19,3},{4,20},{20... | collective-permute-start | bytes 776 | tf_op jit(solution)/shard_map/ppermute | solution.py:526
  2.6 0.5 copy-start

commit v4 on v2

--- a/solution.py
+++ b/solution.py
@@ -461,8 +461,8 @@
 
     project(0)
     attend_block(0)
+    forward(0)
     project(1)
-    forward(0)
     attend_block(1)
     forward(1)
 

time: 98.7 us -> 103 us (1.044)
  Pallas kernels: 93.8 us -> 97.3 us
    pallas_call x1, Pallas kernels: 88 us -> 91.5 us  [chained(): pl.pallas_call(functools.partial(chain_kernel, n_seq, n_sec, n_tp), out_s...]
where the time goes in v4:
time: 103 us; the launch traced here: 102 us
  Pallas kernels  97.3 us (94%)
  local copies, waits for them, and re-layouts  2.11 us (2%)
  waiting for transfers between devices  1.25 us (1%)
  other arithmetic  1.07 us (1%)
    pallas_call x1, Pallas kernels, chained(): pl.pallas_call(functools.partial(chain_kernel, n_seq, n_sec, n_tp), out_s...  91.5 us
    pallas_call x1, Pallas kernels, chained(): pl.pallas_call(lookup_kernel, out_shape=jax.ShapeDtypeStruct((piece, chun...  5.85 us
    unnamed x3, local copies, waits for them, and re-layouts  2.11 us
  transfers between devices with their start and end apart: 1, of which 1 were waited for; matrix products, arithmetic and copies ran while one was open for 1% of the time, Pallas kernels for 0%

profile of v4, /device:TPU:15, one launch (start us, length us, event | category | flops | bytes accessed | tf_op | source)
XLA Modules:
  0.0 102.0 jit_solution(7495753778538766153)
XLA Ops:
  0.0 0.2 collective-permute-start
  0.2 0.3 fusion
  0.6 0.7 pad_maximum_fusion
  1.3 1.2 %collective-permute-done.theirs_ref = s32[64]{0:T(128)S(1)} collective-permute-done((s32[64]{0:T(128)}, s32[64]{0:T(128)S(1)}, u32[]{:S(2)}, u32[]{:S(2)}) %collective-permute-start) | collective-permute-done | bytes 288 | tf_op jit(solution)/shard_map/ppermute | solution.py:506
  2.6 0.0 copy-start
  2.6 0.5 copy-done
  3.1 5.8 %shard_map.55.piece_ref = bf16[32,512]{1,0:T(8,128)(2,1)} custom-call(s32[64]{0:T(128)} %mine_ref.1, s32[64]{0:T(128)} %copy-done, bf16[512,65536]{1,0:T(8,128)(2,1)} %table_ref.1), custom_call_target="tpu_custom_call" | custom-call | tf_op jit(solution)/shard_map/pallas_call | solution.py:507
  9.0 91.5 %shard_map.56 = bf16[1,64,1024]{2,1,0:T(8,128)(2,1)} custom-call(bf16[32,512]{1,0:T(8,128)(2,1)} %shard_map.55.piece_ref, bf16[1,4096]{1,0:T(2,128)(2,1)} %gain_ref.1, f32[128,128]{1,0:T(8,128)} %get-tuple-element.8.cos_ref, f32[128,128]{1,0:T(8,128)} %get-tuple-element.9.sin_ref, bf16[1,2048,1024]{2,1,0:T(8,128)(2,1)} %qkv_ref.1, bf16[1,2048,512]{2,1,0:T(8,128)(2,1)} %outw_ref.1), custom_call_target="tpu_custom_call" | custom-call | tf_op jit(solution)/shard_map/pallas_call | solution.py:527
  100.4 1.6 %copy.7 = bf16[1,64,1024]{2,1,0:T(8,128)(2,1)} copy(bf16[1,64,1024]{2,1,0:T(8,128)(2,1)} %shard_map.56) | data formatting | bytes 262144
  (2 shorter events, 0.0 us)
Async XLA Ops:
  0.0 2.6 %collective-permute-start = (s32[64]{0:T(128)}, s32[64]{0:T(128)S(1)}, u32[]{:S(2)}, u32[]{:S(2)}) collective-permute-start(s32[64]{0:T(128)} %mine_ref.1), channel_id=1, source_target_pairs={{0,16},{16,0},{1,17},{17,1},{2,18},{18,2},{3,19},{19,3},{4,20},{20... | collective-permute-start | bytes 776 | tf_op jit(solution)/shard_map/ppermute | solution.py:506
  2.6 0.5 copy-start
